TPU v7x, 32 devices: a whole 2x2x4 slice. The times are simulated.
32 devices in a mesh: seq: 16 (over z, x, core), dp: 2 (over y).
Axes of the slice: x: 2, y: 2, z: 4, core: 2. Of those that a mesh axis runs over, the one named last changes fastest.
Arguments:
- spectrum: bfloat16 [16, 64, 2, 1025], P('seq', 'dp'), parts along dimension 1, may hold values from -6 to 6
- band_table: int32 [60, 2], replicated, may hold values from 0 to 1024, as said below
- band_weight: bfloat16 [60, 2, 64, 384], replicated, may hold values from -0.5 to 0.5
- qkv_weight: bfloat16 [2, 384, 1152], replicated, may hold values from -1.5 to 1.5
- out_weight: bfloat16 [2, 384, 384], replicated, may hold values from -0.3125 to 0.3125
- ff_in_weight: bfloat16 [2, 384, 768], replicated, may hold values from -0.3125 to 0.3125
- ff_out_weight: bfloat16 [2, 768, 384], replicated, may hold values from -0.21875 to 0.21875
- norm_gains: float32 [6, 384], replicated, may hold values from 0.1 to 1.9
Outputs:
- hidden_out: bfloat16 [16, 64, 60, 384], P('seq', 'dp'), parts along dimension 1
There are 2 independent parts, one for each index of `dp`. A program takes and returns all parts, laid end to end along the dimension named above; an argument that names none is the same for every part. Nothing has to cross between parts.
Inputs may be any that keep to these rules, and one draw needn't show every extreme that they name: `band_table`: row n holds band n's first bin and its number of bins; each band lies inside the 1025 bins and has 2 to 64 bins, the last band exactly 64; bands intersect at low frequencies.
All inputs are finite; a program needn't handle non-finite values.
Results may differ from a plain program's by a relative error of at most 0.017.
Values may be sent and summed in bfloat16 or wider, within the bound.
A program may use at most 128 MiB of HBM per device.

v0:
```python
import functools
import math

import jax
import jax.numpy as jnp
import numpy as np
from jax import lax
from jax.experimental import pallas as pl
from jax.experimental.pallas import tpu as pltpu
from jax.sharding import PartitionSpec as P

HEADS = 8
SPAN = 64


EPSILON = 0.05


def normalize(values, gain_row):
    return (
        values * lax.rsqrt(jnp.mean(values * values, axis=-1, keepdims=True) + EPSILON) * gain_row
    )


def rotate(tensor, positions):
    half_size = tensor.shape[-1] // 2
    frequency = 10000.0 ** (-jnp.arange(half_size, dtype=jnp.float32) / half_size)
    angles = positions[..., None] * frequency
    cosine = jnp.cos(angles)
    sine_part = jnp.sin(angles)
    first_half = tensor[..., :half_size]
    second_half = tensor[..., half_size:]
    return jnp.concatenate(
        [
            first_half * cosine - second_half * sine_part,
            second_half * cosine + first_half * sine_part,
        ],
        axis=-1,
    )


def project(stream, weights, gain_row, positions):
    normed = normalize(stream.astype(jnp.float32), gain_row).astype(jnp.bfloat16)
    mixture = jnp.dot(normed, weights, preferred_element_type=jnp.float32)
    model_width = stream.shape[-1]
    head_shape = stream.shape[:-1] + (HEADS, model_width // HEADS)
    queries = (
        rotate(mixture[..., :model_width].reshape(head_shape), positions)
        .astype(jnp.bfloat16)
        .reshape(stream.shape)
    )
    key_rows = (
        rotate(mixture[..., model_width : 2 * model_width].reshape(head_shape), positions)
        .astype(jnp.bfloat16)
        .reshape(stream.shape)
    )
    value_rows = mixture[..., 2 * model_width :].astype(jnp.bfloat16)
    return (queries, key_rows, value_rows)


def attend_rows(queries, key_rows, value_rows):
    row_count, length, model_width = queries.shape
    head_size = model_width // HEADS
    head_shape = (row_count, length, HEADS, head_size)
    scores = jnp.einsum(
        "rshd,rthd->rhst",
        queries.reshape(head_shape),
        key_rows.reshape(head_shape),
        preferred_element_type=jnp.float32,
    ) / math.sqrt(head_size)
    weights = jax.nn.softmax(scores, axis=-1).astype(jnp.bfloat16)
    context = jnp.einsum(
        "rhst,rthd->rshd",
        weights,
        value_rows.reshape(head_shape),
        preferred_element_type=jnp.float32,
    )
    return context.astype(jnp.bfloat16).reshape(row_count, length, model_width)


def attend_time(queries, key_rows, value_rows):
    context = attend_rows(
        jnp.swapaxes(queries, 0, 1), jnp.swapaxes(key_rows, 0, 1), jnp.swapaxes(value_rows, 0, 1)
    )
    return jnp.swapaxes(context, 0, 1)


def finish(stream, context, weights):
    return (
        stream.astype(jnp.float32) + jnp.dot(context, weights, preferred_element_type=jnp.float32)
    ).astype(jnp.bfloat16)


def feed_forward(stream, weight_in, weight_out, gain_row):
    normed = normalize(stream.astype(jnp.float32), gain_row).astype(jnp.bfloat16)
    active = jax.nn.gelu(
        jnp.dot(normed, weight_in, preferred_element_type=jnp.float32), approximate=True
    ).astype(jnp.bfloat16)
    return (
        stream.astype(jnp.float32) + jnp.dot(active, weight_out, preferred_element_type=jnp.float32)
    ).astype(jnp.bfloat16)


def flatten_items(block):
    return block.reshape(block.shape[0], block.shape[2], block.shape[3])


LANES = 128
PAIRS = HEADS // 2
WIDE = PAIRS * LANES
F32 = jnp.float32
BF16 = jnp.bfloat16
TIME_BANDS = 32
MESH = pl.DeviceIdType.MESH


def fits_batch_plan(spectrum, band_table, band_weight):
    groups = lax.axis_size("seq")
    return (
        spectrum.shape[0] == 1
        and spectrum.shape[1] % groups == 0
        and groups % 16 == 0
        and groups <= 16
        and band_table.shape[0] <= 2 * TIME_BANDS
        and band_table.shape[0] > TIME_BANDS
        and band_weight.shape[3] == HEADS * 48
    )


def rotation_tables(length, head_size, scale):
    half = head_size // 2
    frequency = 10000.0 ** (-np.arange(half, dtype=np.float64) / half)
    angles = np.arange(length, dtype=np.float64)[:, None] * frequency
    cosine = np.zeros((length, LANES), np.float32)
    sine = np.zeros((length, LANES), np.float32)
    for head in range(2):
        for part in range(2):
            at = part * 64 + head * 32
            cosine[:, at : at + half] = np.cos(angles) * scale
            sine[:, at : at + half] = np.sin(angles) * (scale if part else -scale)
    return cosine, sine


def dot(left, right):
    return jnp.dot(left, right, preferred_element_type=F32)


def rms(values, gain):
    mean = jnp.mean(values * values, axis=-1, keepdims=True)
    return values * lax.rsqrt(mean + EPSILON) * gain


def layer(x, tables, gain_a, gain_f, wqkv, wout, wfi, wfo, size, mask, low):
    rows = x.shape[0]
    blocks = rows // size
    cq, sq, ck, sk = tables
    lane = lax.broadcasted_iota(jnp.int32, (1, LANES), 1)
    first = ((lane & 32) == 0).astype(BF16)
    second = ((lane & 32) != 0).astype(BF16)
    normed = rms(x, gain_a).astype(BF16)
    mixture = dot(normed, wqkv)

    def turned(part, cosine, sine):
        swapped = pltpu.roll(part, 64, 1)
        part = part.reshape(blocks, size, LANES) * cosine[None]
        return (part + swapped.reshape(blocks, size, LANES) * sine[None]).astype(BF16)

    columns = []
    for pair in range(PAIRS):
        at = pair * LANES
        q = turned(mixture[:, at : at + LANES], cq, sq)
        k = turned(mixture[:, WIDE + at : WIDE + at + LANES], ck, sk)
        v = mixture[:, 2 * WIDE + at : 2 * WIDE + at + LANES].astype(BF16)
        pieces = []
        for block in range(blocks):
            qb = q[block]
            stacked = jnp.concatenate([qb * first, qb * second], axis=0)
            scores = lax.dot_general(
                k[block], stacked, (((1,), (1,)), ((), ())), preferred_element_type=F32
            )
            scores = jnp.where(mask, scores, low)
            scores = jnp.exp2(scores - jnp.max(scores, axis=0, keepdims=True))
            total = jnp.sum(scores, axis=0, keepdims=True)
            probs = (scores * (1.0 / total)).astype(BF16)
            mixed = lax.dot_general(
                probs,
                v[block * size : (block + 1) * size],
                (((0,), (0,)), ((), ())),
                preferred_element_type=F32,
            )
            pieces.append(jnp.where(lane < 64, mixed[:size], mixed[size:]))
        columns.append(jnp.concatenate(pieces, axis=0).astype(BF16))
    x = x + dot(jnp.concatenate(columns, axis=1), wout)
    normed = rms(x, gain_f).astype(BF16)
    u = dot(normed, wfi)
    c = math.sqrt(2.0 / math.pi)
    act = 0.5 * u * (1.0 + jnp.tanh(u * (c + (c * 0.044715) * (u * u))))
    return x + dot(act.astype(BF16), wfo)


def whole_kernel(
    groups,
    own,
    bands,
    bins,
    table,
    spectrum,
    band_weight,
    qkv,
    out_w,
    ff_in,
    ff_out,
    gains,
    cq0,
    sq0,
    ck0,
    sk0,
    cq1,
    sq1,
    ck1,
    sk1,
    out,
    arrived,
    spec,
    bw,
    raw_qkv,
    raw_out,
    wqkv,
    wout,
    wfi,
    wfo,
    x0,
    x1,
    sending,
    load_sem,
    spec_send,
    spec_recv,
    spec_own,
    send_sem,
    recv_sem,
    own_sem,
):
    me = lax.axis_index("seq")
    padded = 2 * TIME_BANDS
    frames = groups
    width = gains.shape[1]
    loads = [
        pltpu.make_async_copy(qkv, raw_qkv, load_sem.at[0]),
        pltpu.make_async_copy(out_w, raw_out, load_sem.at[1]),
        pltpu.make_async_copy(band_weight, bw, load_sem.at[2]),
        pltpu.make_async_copy(ff_in, wfi, load_sem.at[3]),
        pltpu.make_async_copy(ff_out, wfo, load_sem.at[4]),
    ]
    for load in loads:
        load.start()

    barrier = pltpu.get_barrier_semaphore()

    def greet(k, carry):
        peer = lax.rem(me + k, groups)
        pl.semaphore_signal(barrier, inc=1, device_id={"seq": peer}, device_id_type=MESH)
        return carry

    lax.fori_loop(1, groups, greet, 0)
    pl.semaphore_wait(barrier, groups - 1)

    def spec_copy(peer, slot, sem_slot):
        return pltpu.make_async_remote_copy(
            src_ref=spectrum.at[pl.ds(peer * own, own)],
            dst_ref=arrived.at[slot],
            send_sem=spec_send.at[peer],
            recv_sem=spec_recv.at[sem_slot],
            device_id={"seq": peer},
            device_id_type=MESH,
        )

    def spec_start(k, carry):
        peer = lax.rem(me + k, groups)
        spec_copy(peer, me, me).start()
        return carry

    lax.fori_loop(1, groups, spec_start, 0)
    mine = pltpu.make_async_copy(
        spectrum.at[pl.ds(me * own, own)], arrived.at[me], spec_own.at[0]
    )
    mine.start()

    col = lax.broadcasted_iota(jnp.int32, (1, WIDE), 1)
    pair, rest = col >> 7, col & 127
    part, head, at = rest >> 6, (rest >> 5) & 1, rest & 31
    source = jnp.where(at < 24, pair * 96 + head * 48 + part * 24 + at, -1)
    row = lax.broadcasted_iota(jnp.int32, (width, WIDE), 0)
    spread_qk = (row == source).astype(F32).astype(BF16)
    source = jnp.where((col & 63) < 48, (col >> 6) * 48 + (col & 63), -1)
    spread_v = (row == source).astype(F32).astype(BF16)
    col = lax.broadcasted_iota(jnp.int32, (WIDE, 1), 0)
    source = jnp.where((col & 63) < 48, (col >> 6) * 48 + (col & 63), -1)
    row = lax.broadcasted_iota(jnp.int32, (WIDE, width), 1)
    spread_o = (row == source).astype(F32).astype(BF16)
    loads[0].wait()
    loads[1].wait()
    for sub in range(2):
        for block in range(3):
            spread = spread_v if block == 2 else spread_qk
            wqkv[sub, :, block * WIDE : (block + 1) * WIDE] = dot(
                raw_qkv[sub, :, block * width : (block + 1) * width], spread
            ).astype(BF16)
        wout[sub] = dot(spread_o, raw_out[sub]).astype(BF16)

    mine.wait()

    def spec_wait(k, carry):
        peer = lax.rem(me + k, groups)
        copy = spec_copy(peer, peer, peer)
        copy.wait_send()
        copy.wait_recv()
        return carry

    lax.fori_loop(1, groups, spec_wait, 0)
    for f in range(frames):
        for b in range(own):
            both = arrived[f, b].astype(F32)
            at = b * frames + f
            spec[at : at + 1, 0:bins] = both[0:1]
            at = (own + b) * frames + f
            spec[at : at + 1, 0:bins] = both[1:2]

    loads[2].wait()
    lane = lax.broadcasted_iota(jnp.int32, (1, LANES), 1)
    gain0 = gains[0:1, :]

    def scatter(n, values):
        for b in range(own):
            for piece in range(width // LANES):
                x0[piece, pl.ds(b * frames * padded + n, frames, stride=padded), :] = values[
                    b * frames : (b + 1) * frames, piece * LANES : (piece + 1) * LANES
                ]

    def embed(n, carry):
        start = table[n, 0]
        count = table[n, 1]
        amount = jnp.full((1, LANES), start, jnp.int32)
        tiles = [
            spec[:, i * LANES : (i + 1) * LANES] for i in range(spec.shape[1] // LANES)
        ]
        for bit in range(3, -1, -1):
            step = 1 << bit
            if len(tiles) > step:
                chosen = (amount & (LANES << bit)) != 0
                tiles = [
                    jnp.where(chosen, tiles[i + step], tiles[i]) if i + step < len(tiles) else tiles[i]
                    for i in range(min(len(tiles), step + 1))
                ]
        window = jnp.concatenate(tiles[:2], axis=1)
        for bit in range(7):
            moved = pltpu.roll(window, 256 - (1 << bit), 1)
            chosen = (jnp.full((1, 256), start, jnp.int32) & (1 << bit)) != 0
            window = jnp.where(chosen, moved, window)
        count_rows = own * frames
        high = pltpu.roll(window[count_rows:, :LANES], 64, 1)
        picked = jnp.where(lane < 64, window[:count_rows, :LANES], high)
        picked = jnp.where((lane & 63) < count, picked, 0.0).astype(BF16)
        scatter(n, rms(dot(picked, bw[n]), gain0))
        return carry

    lax.fori_loop(0, bands, embed, 0, unroll=4)
    for n in range(bands, padded):
        scatter(n, jnp.zeros((own * frames, width), F32))

    loads[3].wait()
    loads[4].wait()
    rows = 512
    band_mask = lax.broadcasted_iota(jnp.int32, (padded, 2 * padded), 0) < bands
    small = 8 * frames
    time_mask = (lax.broadcasted_iota(jnp.int32, (small, 2 * small), 0) & 7) == (
        lax.broadcasted_iota(jnp.int32, (small, 2 * small), 1) & 7
    )

    def out_copy(peer, b, part, slot):
        return pltpu.make_async_remote_copy(
            src_ref=sending.at[b, part, peer],
            dst_ref=out.at[slot * own + b, pl.ds(part * TIME_BANDS, TIME_BANDS)],
            send_sem=send_sem.at[b, part, peer],
            recv_sem=recv_sem.at[b, part, slot],
            device_id={"seq": peer},
            device_id_type=MESH,
        )

    def own_copy(b, part):
        return pltpu.make_async_copy(
            sending.at[b, part, me],
            out.at[me * own + b, pl.ds(part * TIME_BANDS, TIME_BANDS)],
            own_sem.at[b, part],
        )

    def one_row(b, carry):
        def band_chunk(chunk, carry):
            at = pl.multiple_of(b * frames * padded + chunk * rows, rows)
            x = jnp.concatenate(
                [x0[piece, pl.ds(at, rows), :] for piece in range(width // LANES)], axis=1
            )
            x = layer(
                x,
                (cq0[...], sq0[...], ck0[...], sk0[...]),
                gains[1:2, :],
                gains[2:3, :],
                wqkv[0],
                wout[0],
                wfi[0],
                wfo[0],
                padded,
                band_mask,
                -1e30,
            )
            count = rows // padded
            x1[b, pl.ds(chunk * count, count)] = x.reshape(count, padded, width)
            return carry

        lax.fori_loop(0, frames * padded // rows, band_chunk, 0)

        def time_chunk(part, carry):
            n0 = part * TIME_BANDS
            x = jnp.concatenate(
                [
                    x1[b, :, pl.ds(pl.multiple_of(n0 + 8 * g, 8), 8), :].reshape(small, width)
                    for g in range(TIME_BANDS // 8)
                ],
                axis=0,
            )
            x = layer(
                x,
                (cq1[...], sq1[...], ck1[...], sk1[...]),
                gains[3:4, :],
                gains[4:5, :],
                wqkv[1],
                wout[1],
                wfi[1],
                wfo[1],
                small,
                time_mask,
                -1e30,
            )
            y = rms(x, gains[5:6, :])
            y = jnp.concatenate(
                [
                    y[g * small : (g + 1) * small].reshape(frames, 8, width)
                    for g in range(TIME_BANDS // 8)
                ],
                axis=1,
            )
            sending[b, part] = y.astype(BF16)

            def start(k, carry):
                peer = lax.rem(me + k, groups)
                out_copy(peer, b, part, me).start()
                return carry

            lax.fori_loop(1, groups, start, 0)
            own_copy(b, part).start()
            return carry

        lax.fori_loop(0, padded // TIME_BANDS, time_chunk, 0)
        return carry

    lax.fori_loop(0, own, one_row, 0)

    def finish_all(i, carry):
        b, part = i // 2, lax.rem(i, 2)

        def one(k, carry):
            peer = lax.rem(me + k, groups)
            copy = out_copy(peer, b, part, peer)
            copy.wait_send()
            copy.wait_recv()
            return carry

        lax.fori_loop(1, groups, one, 0)
        own_copy(b, part).wait()
        return carry

    lax.fori_loop(0, own * 2, finish_all, 0)


def batch_plan(
    spectrum,
    band_table,
    band_weight,
    qkv_weight,
    out_weight,
    ff_in_weight,
    ff_out_weight,
    norm_gains,
):
    groups = lax.axis_size("seq")
    _, batch_size, channels, bins = spectrum.shape
    bands = band_table.shape[0]
    width = band_weight.shape[3]
    hidden = ff_in_weight.shape[2]
    own = batch_size // groups
    padded = 2 * TIME_BANDS
    bins_padded = -(-bins // LANES) * LANES
    head_size = width // HEADS
    scale = math.log2(math.e) / math.sqrt(head_size)
    tables = []
    for length, repeat in ((padded, 1), (groups, 8)):
        for factor in (scale, 1.0):
            for piece in rotation_tables(length, head_size, factor):
                tables.append(np.repeat(piece, repeat, axis=0))
    vmem = pl.BlockSpec(memory_space=pltpu.VMEM)
    anywhere = pl.BlockSpec(memory_space=pl.ANY)
    dma = pltpu.SemaphoreType.DMA
    out = pl.pallas_call(
        functools.partial(whole_kernel, groups, own, bands, bins),
        out_shape=jax.ShapeDtypeStruct((batch_size, padded, width), BF16),
        in_specs=[pl.BlockSpec(memory_space=pltpu.SMEM)] + [anywhere] * 6 + [vmem] * 9,
        out_specs=anywhere,
        scratch_shapes=[
            pltpu.VMEM((groups, own, channels, bins), BF16),
            pltpu.VMEM((channels * own * groups, bins_padded), F32),
            pltpu.VMEM((bands, channels * SPAN, width), BF16),
            pltpu.VMEM((2, width, 3 * width), BF16),
            pltpu.VMEM((2, width, width), BF16),
            pltpu.VMEM((2, width, 3 * WIDE), BF16),
            pltpu.VMEM((2, WIDE, width), BF16),
            pltpu.VMEM((2, width, hidden), BF16),
            pltpu.VMEM((2, hidden, width), BF16),
            pltpu.VMEM((width // LANES, own * groups * padded, LANES), F32),
            pltpu.VMEM((own, groups, padded, width), F32),
            pltpu.VMEM((own, 2, groups, TIME_BANDS, width), BF16),
            dma((5,)),
            dma((groups,)),
            dma((groups,)),
            dma((1,)),
            dma((own, 2, groups)),
            dma((own, 2, groups)),
            dma((own, 2)),
        ],
        compiler_params=pltpu.CompilerParams(collective_id=0, has_side_effects=True),
    )(
        band_table,
        spectrum.reshape(batch_size, channels, bins),
        band_weight.reshape(bands, channels * SPAN, width),
        qkv_weight,
        out_weight,
        ff_in_weight,
        ff_out_weight,
        norm_gains,
        *[jnp.asarray(t) for t in tables],
    )
    return out[None, :, :bands]


def body(
    spectrum,
    band_table,
    band_weight,
    qkv_weight,
    out_weight,
    ff_in_weight,
    ff_out_weight,
    norm_gains,
):
    frame_count, batch_size, channel_count, bin_count = spectrum.shape
    band_count = band_table.shape[0]
    if fits_batch_plan(spectrum, band_table, band_weight):
        return batch_plan(
            spectrum,
            band_table,
            band_weight,
            qkv_weight,
            out_weight,
            ff_in_weight,
            ff_out_weight,
            norm_gains,
        )
    offsets = jnp.arange(SPAN, dtype=jnp.int32)
    targets = (band_table[:, 0:1] + offsets[None, :]).reshape(-1)
    valid = (offsets[None, :] < band_table[:, 1:2]).reshape(-1)
    chosen = (
        (jnp.arange(bin_count, dtype=jnp.int32)[:, None] == targets[None, :]) & valid[None, :]
    ).astype(jnp.bfloat16)
    features = jnp.einsum(
        "fbcq,qm->fbcm", spectrum, chosen, preferred_element_type=jnp.float32
    ).astype(jnp.bfloat16)
    features = features.reshape(frame_count, batch_size, channel_count, band_count, SPAN)
    embedded = jnp.einsum(
        "fbcnj,ncjd->fbnd", features, band_weight, preferred_element_type=jnp.float32
    )
    model_width = embedded.shape[-1]
    stream = normalize(embedded, norm_gains[0]).astype(jnp.bfloat16)
    stream = stream.reshape(frame_count * batch_size, band_count, model_width)
    band_positions = jnp.arange(band_count, dtype=jnp.float32).reshape(1, band_count, 1)
    triple = project(stream, qkv_weight[0], norm_gains[1], band_positions)
    stream = finish(stream, attend_rows(triple[0], triple[1], triple[2]), out_weight[0])
    stream = feed_forward(stream, ff_in_weight[0], ff_out_weight[0], norm_gains[2])
    groups = lax.axis_size("seq")
    pair_count = batch_size * band_count
    per_group = pair_count // groups
    stream = stream.reshape(frame_count, groups, per_group, model_width)
    block = lax.all_to_all(stream, "seq", split_axis=1, concat_axis=0, tiled=True)
    flat = flatten_items(block)
    length = flat.shape[0]
    frame_positions = jnp.arange(length, dtype=jnp.float32).reshape(length, 1, 1)
    parts = project(flat, qkv_weight[1], norm_gains[3], frame_positions)
    mixed_block = finish(flat, attend_time(parts[0], parts[1], parts[2]), out_weight[1])
    result_block = feed_forward(mixed_block, ff_in_weight[1], ff_out_weight[1], norm_gains[4])
    regrouped = result_block.reshape(block.shape)
    stream = lax.all_to_all(regrouped, "seq", split_axis=0, concat_axis=1, tiled=True)
    stream = stream.reshape(frame_count, pair_count, model_width)
    result = normalize(stream.astype(jnp.float32), norm_gains[5]).astype(jnp.bfloat16)
    return result.reshape(frame_count, batch_size, band_count, model_width)


def solution(mesh):
    in_specs = (P("seq", "dp", None, None), P(), P(), P(), P(), P(), P(), P())
    out_specs = P("seq", "dp", None, None)
    return jax.shard_map(body, mesh=mesh, in_specs=in_specs, out_specs=out_specs, check_vma=False)
```

profile of v0, /device:TPU:9, one launch (start us, length us, event | category | flops | bytes accessed | tf_op | source)
XLA Modules:
  0.0 103.3 jit_solution(18222390751364561179)
XLA Ops:
  0.0 1.4 %copy.17.table = s32[60,2]{1,0:T(8,128)} copy(s32[60,2]{0,1:T(2,128)} %param.17) | data formatting | bytes 960 | tf_op args[1]
  1.4 98.4 %shard_map.154 = bf16[32,64,384]{2,1,0:T(8,128)(2,1)} custom-call(s32[60,2]{1,0:T(8,128)} %copy.17.table, bf16[32,2,1025]{2,1,0:T(2,128)(2,1)} %bitcast.5, bf16[60,128,384]{2,1,0:T(8,128)(2,1)} %bitcast.4, bf16[2,384,1152]{2,1,0:T(8,128)(2,1)} %qkv.1, bf16[2,384,384]{2,1,0:T(8,128)(2,1)} %out_w.1, bf16[2,384,768]{2,1,0:T(8,128)(2,1)} %ff_in.1, ...), custom_call_target="tpu_custom_call" | custom-call | tf_op jit(solution)/shard_map/pallas_call | solution.py:512
  99.8 1.6 %slice_bitcast_fusion = bf16[1,32,60,384]{3,2,1,0:T(8,128)(2,1)S(1)} fusion(bf16[32,64,384]{2,1,0:T(8,128)(2,1)} %shard_map.154), kind=kLoop, calls=%fused_computation | loop fusion | bytes 2949120 | tf_op jit(solution)/shard_map/broadcast_in_dim | solution.py:550
  101.3 2.0 %copy.18 = bf16[1,32,60,384]{3,1,2,0:T(8,128)(2,1)} copy(bf16[1,32,60,384]{3,2,1,0:T(8,128)(2,1)S(1)} %slice_bitcast_fusion) | data formatting | bytes 2949120 | tf_op jit(solution)/shard_map/broadcast_in_dim | solution.py:550
where the time goes:
time: 104 us; the launch traced here: 103 us
  Pallas kernels  98.4 us (95%)
  local copies, waits for them, and re-layouts  4.93 us (5%)
    pallas_call x1, Pallas kernels, batch_plan(): pl.pallas_call(functools.partial(whole_kernel, groups, own, bands, bins),...  98.4 us
    broadcast_in_dim x2, local copies, waits for them, and re-layouts, batch_plan(): return out[None, :, :bands]  3.54 us

commit v1 on v0

--- a/solution.py
+++ b/solution.py
@@ -123,6 +123,9 @@
         and groups <= 16
         and band_table.shape[0] <= 2 * TIME_BANDS
         and band_table.shape[0] > TIME_BANDS
+        and band_table.shape[0] % 4 == 0
+        and SPAN == 64
+        and spectrum.shape[2] == 2
         and band_weight.shape[3] == HEADS * 48
     )
 
@@ -222,6 +225,7 @@
     out,
     arrived,
     spec,
+    feats,
     bw,
     raw_qkv,
     raw_out,
@@ -280,6 +284,8 @@
         return carry
 
     lax.fori_loop(1, groups, spec_start, 0)
+    tail = bins // LANES * LANES
+    spec[:, tail:] = jnp.zeros((spec.shape[0], spec.shape[1] - tail), F32)
     mine = pltpu.make_async_copy(
         spectrum.at[pl.ds(me * own, own)], arrived.at[me], spec_own.at[0]
     )
@@ -336,41 +342,48 @@
                     b * frames : (b + 1) * frames, piece * LANES : (piece + 1) * LANES
                 ]
 
-    def embed(n, carry):
-        start = table[n, 0]
-        count = table[n, 1]
-        amount = jnp.full((1, LANES), start, jnp.int32)
-        tiles = [
-            spec[:, i * LANES : (i + 1) * LANES] for i in range(spec.shape[1] // LANES)
-        ]
-        for bit in range(3, -1, -1):
-            step = 1 << bit
-            if len(tiles) > step:
-                chosen = (amount & (LANES << bit)) != 0
-                tiles = [
-                    jnp.where(chosen, tiles[i + step], tiles[i]) if i + step < len(tiles) else tiles[i]
-                    for i in range(min(len(tiles), step + 1))
-                ]
-        window = jnp.concatenate(tiles[:2], axis=1)
-        for bit in range(7):
-            moved = pltpu.roll(window, 256 - (1 << bit), 1)
-            chosen = (jnp.full((1, 256), start, jnp.int32) & (1 << bit)) != 0
-            window = jnp.where(chosen, moved, window)
-        count_rows = own * frames
-        high = pltpu.roll(window[count_rows:, :LANES], 64, 1)
-        picked = jnp.where(lane < 64, window[:count_rows, :LANES], high)
-        picked = jnp.where((lane & 63) < count, picked, 0.0).astype(BF16)
-        scatter(n, rms(dot(picked, bw[n]), gain0))
+    quad = 4 * SPAN
+    offset = lax.broadcasted_iota(jnp.int32, (1, quad), 1) & (SPAN - 1)
+    owner = lax.broadcasted_iota(jnp.int32, (1, quad), 1) // SPAN
+    lines = spec[...].astype(BF16)
+    bin_row = lax.broadcasted_iota(jnp.int32, (spec.shape[1], quad), 0)
+
+    def pick(m, carry):
+        target = jnp.full((1, quad), -1, jnp.int32)
+        for i in range(4):
+            start = jnp.full((1, quad), table[0, 4 * m + i], jnp.int32)
+            count = jnp.full((1, quad), table[1, 4 * m + i], jnp.int32)
+            inside = (owner == i) & (offset < count)
+            target = jnp.where(inside, start + offset, target)
+        chosen = (bin_row == target).astype(F32).astype(BF16)
+        feats[m] = dot(lines, chosen)
         return carry
 
-    lax.fori_loop(0, bands, embed, 0, unroll=4)
+    lax.fori_loop(0, bands // 4, pick, 0, unroll=3)
+    half = own * frames
+
+    def embed(m, carry):
+        for i in range(2):
+            low = feats[m, :half, i * LANES : (i + 1) * LANES]
+            high = feats[m, half:, i * LANES : (i + 1) * LANES]
+            even = jnp.where(lane < SPAN, low, pltpu.roll(high, SPAN, 1)).astype(BF16)
+            odd = jnp.where(lane < SPAN, pltpu.roll(low, SPAN, 1), high).astype(BF16)
+            n = 4 * m + 2 * i
+            scatter(n, rms(dot(even, bw[n]), gain0))
+            scatter(n + 1, rms(dot(odd, bw[n + 1]), gain0))
+        return carry
+
+    lax.fori_loop(0, bands // 4, embed, 0, unroll=3)
     for n in range(bands, padded):
         scatter(n, jnp.zeros((own * frames, width), F32))
 
     loads[3].wait()
     loads[4].wait()
     rows = 512
-    band_mask = lax.broadcasted_iota(jnp.int32, (padded, 2 * padded), 0) < bands
+    double = 2 * padded
+    key = lax.broadcasted_iota(jnp.int32, (double, 2 * double), 0)
+    query = lax.broadcasted_iota(jnp.int32, (double, 2 * double), 1)
+    band_mask = (((key ^ query) & padded) == 0) & ((key & (padded - 1)) < bands)
     small = 8 * frames
     time_mask = (lax.broadcasted_iota(jnp.int32, (small, 2 * small), 0) & 7) == (
         lax.broadcasted_iota(jnp.int32, (small, 2 * small), 1) & 7
@@ -408,7 +421,7 @@
                 wout[0],
                 wfi[0],
                 wfo[0],
-                padded,
+                double,
                 band_mask,
                 -1e30,
             )
@@ -502,10 +515,12 @@
     head_size = width // HEADS
     scale = math.log2(math.e) / math.sqrt(head_size)
     tables = []
-    for length, repeat in ((padded, 1), (groups, 8)):
-        for factor in (scale, 1.0):
-            for piece in rotation_tables(length, head_size, factor):
-                tables.append(np.repeat(piece, repeat, axis=0))
+    for factor in (scale, 1.0):
+        for piece in rotation_tables(padded, head_size, factor):
+            tables.append(np.tile(piece, (2, 1)))
+    for factor in (scale, 1.0):
+        for piece in rotation_tables(groups, head_size, factor):
+            tables.append(np.repeat(piece, 8, axis=0))
     vmem = pl.BlockSpec(memory_space=pltpu.VMEM)
     anywhere = pl.BlockSpec(memory_space=pl.ANY)
     dma = pltpu.SemaphoreType.DMA
@@ -517,6 +532,7 @@
         scratch_shapes=[
             pltpu.VMEM((groups, own, channels, bins), BF16),
             pltpu.VMEM((channels * own * groups, bins_padded), F32),
+            pltpu.VMEM((bands // 4, channels * own * groups, 4 * SPAN), F32),
             pltpu.VMEM((bands, channels * SPAN, width), BF16),
             pltpu.VMEM((2, width, 3 * width), BF16),
             pltpu.VMEM((2, width, width), BF16),
@@ -537,7 +553,7 @@
         ],
         compiler_params=pltpu.CompilerParams(collective_id=0, has_side_effects=True),
     )(
-        band_table,
+        band_table.T,
         spectrum.reshape(batch_size, channels, bins),
         band_weight.reshape(bands, channels * SPAN, width),
         qkv_weight,

time: 104 us -> 68.8 us (0.66)
  Pallas kernels: 98.4 us -> 65.1 us
  local copies, waits for them, and re-layouts: 4.93 us -> 3.54 us
    pallas_call x1, Pallas kernels: 98.4 us -> 65.1 us  [batch_plan(): pl.pallas_call(functools.partial(whole_kernel, groups, own, bands, bins),...]
    unnamed x1 -> x0, local copies, waits for them, and re-layouts: 1.39 us -> none
where the time goes in v1:
time: 68.8 us; the launch traced here: 68.6 us
  Pallas kernels  65.1 us (95%)
  local copies, waits for them, and re-layouts  3.54 us (5%)
    pallas_call x1, Pallas kernels, batch_plan(): pl.pallas_call(functools.partial(whole_kernel, groups, own, bands, bins),...  65.1 us
    broadcast_in_dim x2, local copies, waits for them, and re-layouts, batch_plan(): return out[None, :, :bands]  3.54 us

profile of v1, /device:TPU:9, one launch (start us, length us, event | category | flops | bytes accessed | tf_op | source)
XLA Modules:
  0.0 68.6 jit_solution(17831133721078234583)
XLA Ops:
  0.0 65.1 %shard_map.154 = bf16[32,64,384]{2,1,0:T(8,128)(2,1)} custom-call(s32[2,60]{1,0:T(2,128)} %bitcast.7, bf16[32,2,1025]{2,1,0:T(2,128)(2,1)} %bitcast.6, bf16[60,128,384]{2,1,0:T(8,128)(2,1)} %bitcast.5, bf16[2,384,1152]{2,1,0:T(8,128)(2,1)} %qkv.1, bf16[2,384,384]{2,1,0:T(8,128)(2,1)} %out_w.1, bf16[2,384,768]{2,1,0:T(8,128)(2,1)} %ff_in.1, ...), custom_call_target="tpu_custom_call" | custom-call | tf_op jit(solution)/shard_map/pallas_call | solution.py:527
  65.1 1.6 %slice_bitcast_fusion = bf16[1,32,60,384]{3,2,1,0:T(8,128)(2,1)S(1)} fusion(bf16[32,64,384]{2,1,0:T(8,128)(2,1)} %shard_map.154), kind=kLoop, calls=%fused_computation | loop fusion | bytes 2949120 | tf_op jit(solution)/shard_map/broadcast_in_dim | solution.py:566
  66.7 2.0 %copy.17 = bf16[1,32,60,384]{3,1,2,0:T(8,128)(2,1)} copy(bf16[1,32,60,384]{3,2,1,0:T(8,128)(2,1)S(1)} %slice_bitcast_fusion) | data formatting | bytes 2949120 | tf_op jit(solution)/shard_map/broadcast_in_dim | solution.py:566

commit v2 on v1

--- a/solution.py
+++ b/solution.py
@@ -110,7 +110,9 @@
 WIDE = PAIRS * LANES
 F32 = jnp.float32
 BF16 = jnp.bfloat16
-TIME_BANDS = 32
+TIME_BANDS = 16
+PADDED = 64
+PARTS = PADDED // TIME_BANDS
 MESH = pl.DeviceIdType.MESH
 
 
@@ -121,7 +123,7 @@
         and spectrum.shape[1] % groups == 0
         and groups % 16 == 0
         and groups <= 16
-        and band_table.shape[0] <= 2 * TIME_BANDS
+        and band_table.shape[0] <= PADDED
         and band_table.shape[0] > TIME_BANDS
         and band_table.shape[0] % 4 == 0
         and SPAN == 64
@@ -245,7 +247,7 @@
     own_sem,
 ):
     me = lax.axis_index("seq")
-    padded = 2 * TIME_BANDS
+    padded = PADDED
     frames = groups
     width = gains.shape[1]
     loads = [
@@ -478,7 +480,7 @@
     lax.fori_loop(0, own, one_row, 0)
 
     def finish_all(i, carry):
-        b, part = i // 2, lax.rem(i, 2)
+        b, part = i // PARTS, lax.rem(i, PARTS)
 
         def one(k, carry):
             peer = lax.rem(me + k, groups)
@@ -491,7 +493,7 @@
         own_copy(b, part).wait()
         return carry
 
-    lax.fori_loop(0, own * 2, finish_all, 0)
+    lax.fori_loop(0, own * PARTS, finish_all, 0)
 
 
 def batch_plan(
@@ -510,7 +512,7 @@
     width = band_weight.shape[3]
     hidden = ff_in_weight.shape[2]
     own = batch_size // groups
-    padded = 2 * TIME_BANDS
+    padded = PADDED
     bins_padded = -(-bins // LANES) * LANES
     head_size = width // HEADS
     scale = math.log2(math.e) / math.sqrt(head_size)
@@ -542,14 +544,14 @@
             pltpu.VMEM((2, hidden, width), BF16),
             pltpu.VMEM((width // LANES, own * groups * padded, LANES), F32),
             pltpu.VMEM((own, groups, padded, width), F32),
-            pltpu.VMEM((own, 2, groups, TIME_BANDS, width), BF16),
+            pltpu.VMEM((own, PARTS, groups, TIME_BANDS, width), BF16),
             dma((5,)),
             dma((groups,)),
             dma((groups,)),
             dma((1,)),
-            dma((own, 2, groups)),
-            dma((own, 2, groups)),
-            dma((own, 2)),
+            dma((own, PARTS, groups)),
+            dma((own, PARTS, groups)),
+            dma((own, PARTS)),
         ],
         compiler_params=pltpu.CompilerParams(collective_id=0, has_side_effects=True),
     )(

time: 68.8 us -> 70.2 us (1.020); the launches traced: 68.6 us -> 68.9 us
  no operation moved by 1% of the time
where the time goes in v2:
time: 70.2 us; the launch traced here: 68.9 us
  Pallas kernels  65.3 us (93%)
  local copies, waits for them, and re-layouts  3.54 us (5%)
    pallas_call x1, Pallas kernels, batch_plan(): pl.pallas_call(functools.partial(whole_kernel, groups, own, bands, bins),...  65.3 us
    broadcast_in_dim x2, local copies, waits for them, and re-layouts, batch_plan(): return out[None, :, :bands]  3.54 us

profile of v2, /device:TPU:9, one launch (start us, length us, event | category | flops | bytes accessed | tf_op | source)
XLA Modules:
  0.0 68.9 jit_solution(3136825563369523533)
XLA Ops:
  0.0 65.3 %shard_map.154 = bf16[32,64,384]{2,1,0:T(8,128)(2,1)} custom-call(s32[2,60]{1,0:T(2,128)} %bitcast.7, bf16[32,2,1025]{2,1,0:T(2,128)(2,1)} %bitcast.6, bf16[60,128,384]{2,1,0:T(8,128)(2,1)} %bitcast.5, bf16[2,384,1152]{2,1,0:T(8,128)(2,1)} %qkv.1, bf16[2,384,384]{2,1,0:T(8,128)(2,1)} %out_w.1, bf16[2,384,768]{2,1,0:T(8,128)(2,1)} %ff_in.1, ...), custom_call_target="tpu_custom_call" | custom-call | tf_op jit(solution)/shard_map/pallas_call | solution.py:529
  65.3 1.6 %slice_bitcast_fusion = bf16[1,32,60,384]{3,2,1,0:T(8,128)(2,1)S(1)} fusion(bf16[32,64,384]{2,1,0:T(8,128)(2,1)} %shard_map.154), kind=kLoop, calls=%fused_computation | loop fusion | bytes 2949120 | tf_op jit(solution)/shard_map/broadcast_in_dim | solution.py:568
  66.9 2.0 %copy.17 = bf16[1,32,60,384]{3,1,2,0:T(8,128)(2,1)} copy(bf16[1,32,60,384]{3,2,1,0:T(8,128)(2,1)S(1)} %slice_bitcast_fusion) | data formatting | bytes 2949120 | tf_op jit(solution)/shard_map/broadcast_in_dim | solution.py:568
